TPU v7x, 16 devices: a 4x2x1 block of a 4x4x8 slice. The times are simulated.
16 devices in a mesh: dp: 2 (over y, z), cp: 8 (over x, core).
Axes of the slice: x: 4, y: 2, z: 1, core: 2. Of those that a mesh axis runs over, the one named last changes fastest.
The devices are a block of a 4x4x8 slice.
Arguments:
- x_tok: bfloat16 [128, 3584], P(('dp', 'cp')), parts along dimension 0
- prompt_lens: int32 [128], P('dp'), parts along dimension 0
- k_cache: bfloat16 [128, 512, 4, 128], P('dp', 'cp'), parts along dimension 0
- v_cache: bfloat16 [128, 512, 4, 128], P('dp', 'cp'), parts along dimension 0
- norm_gain: bfloat16 [3584], replicated
- w_q: bfloat16 [3584, 3584], replicated
- b_q: bfloat16 [3584], replicated
- w_k: bfloat16 [3584, 512], replicated
- b_k: bfloat16 [512], replicated
- w_v: bfloat16 [3584, 512], replicated
- b_v: bfloat16 [512], replicated
- w_o: bfloat16 [3584, 3584], replicated
Outputs:
- output 1: bfloat16 [128, 3584], P(('dp', 'cp')), parts along dimension 0
- output 2: bfloat16 [128, 512, 4, 128], P(('dp', 'cp')), parts along dimension 0
- output 3: bfloat16 [128, 512, 4, 128], P(('dp', 'cp')), parts along dimension 0
There are 2 independent parts. A program takes and returns all parts, laid end to end along the dimension named above; an argument that names none is the same for every part.
All inputs are finite; a program needn't handle non-finite values.
Results may differ from a plain program's by a relative error of at most 0.00931332.
Values are sent between devices in bfloat16 or wider.
A program may use at most 768 MiB of HBM per device.

v0:
```python
import jax
import jax.numpy as jnp
from jax import lax
from jax.sharding import PartitionSpec as P

RMS_EPS = 1e-6
ROPE_THETA = 1000000.0


def rotary(vectors, positions):
    head_dim = vectors.shape[-1]
    half_dim = head_dim // 2
    inv_freq = jnp.power(ROPE_THETA, -(jnp.arange(half_dim, dtype=jnp.float32) * 2.0 / head_dim))
    angle = positions.astype(jnp.float32)[:, None, None] * inv_freq
    cos_t = jnp.cos(angle)
    sin_t = jnp.sin(angle)
    first = vectors[..., :half_dim]
    second = vectors[..., half_dim:]
    return jnp.concatenate([first * cos_t - second * sin_t, second * cos_t + first * sin_t], axis=-1)


def project(x_tok, positions, norm_gain, w_q, b_q, w_k, b_k, w_v, b_v, head_dim):
    rows = x_tok.shape[0]
    x_wide = x_tok.astype(jnp.float32)
    mean_sq = jnp.mean(x_wide * x_wide, axis=-1, keepdims=True)
    normed = (x_wide * lax.rsqrt(mean_sq + RMS_EPS) * norm_gain.astype(jnp.float32)).astype(jnp.bfloat16)
    query = jnp.dot(normed, w_q, preferred_element_type=jnp.float32) + b_q.astype(jnp.float32)
    query = rotary(query.reshape(rows, -1, head_dim), positions).astype(jnp.bfloat16)
    key_new = jnp.dot(normed, w_k, preferred_element_type=jnp.float32) + b_k.astype(jnp.float32)
    key_new = rotary(key_new.reshape(rows, -1, head_dim), positions).astype(jnp.bfloat16)
    value_new = jnp.dot(normed, w_v, preferred_element_type=jnp.float32) + b_v.astype(jnp.float32)
    value_new = value_new.reshape(rows, -1, head_dim).astype(jnp.bfloat16)
    return query, key_new, value_new


def decode_local(x_tok, positions, keys_old, vals_old, norm_gain, w_q, b_q, w_k, b_k, w_v, b_v, w_o):
    rows, seq_len, kv_heads, head_dim = keys_old.shape
    query, key_new, value_new = project(x_tok, positions, norm_gain, w_q, b_q, w_k, b_k, w_v, b_v, head_dim)
    heads = query.shape[1]
    group = heads // kv_heads
    slot_idx = lax.broadcasted_iota(jnp.int32, (1, seq_len, 1, 1), 1)
    pos_col = positions[:, None, None, None]
    zero_val = jnp.zeros((), jnp.bfloat16)
    keys_all = jnp.where(slot_idx < pos_col, keys_old, jnp.where(slot_idx == pos_col, key_new[:, None], zero_val))
    vals_all = jnp.where(slot_idx < pos_col, vals_old, jnp.where(slot_idx == pos_col, value_new[:, None], zero_val))
    scores = jnp.einsum('bkgd,bskd->bkgs', query.reshape(rows, kv_heads, group, head_dim), keys_all, preferred_element_type=jnp.float32) * (head_dim ** -0.5)
    valid = lax.broadcasted_iota(jnp.int32, (1, 1, 1, seq_len), 3) <= pos_col
    scores = jnp.where(valid, scores, -1e30)
    row_max = jnp.max(scores, axis=-1, keepdims=True)
    weights = jnp.exp(scores - row_max)
    weight_sum = jnp.sum(weights, axis=-1, keepdims=True)
    mixed = jnp.einsum('bkgs,bskd->bkgd', weights.astype(jnp.bfloat16), vals_all, preferred_element_type=jnp.float32) / weight_sum
    attended = mixed.reshape(rows, heads * head_dim).astype(jnp.bfloat16)
    y_out = (x_tok.astype(jnp.float32) + jnp.dot(attended, w_o, preferred_element_type=jnp.float32)).astype(jnp.bfloat16)
    return y_out, keys_all, vals_all


def solution(mesh):
    batch_spec = P(('dp', 'cp'))
    seq_spec = P('dp', 'cp')
    whole = P()

    def per_device(x_tok, prompt_lens, k_cache, v_cache, norm_gain, w_q, b_q, w_k, b_k, w_v, b_v, w_o):
        rows = x_tok.shape[0]
        first_row = lax.axis_index('cp') * rows
        positions = lax.dynamic_slice_in_dim(prompt_lens, first_row, rows)
        keys_old = lax.all_to_all(k_cache, 'cp', 0, 1, tiled=True)
        vals_old = lax.all_to_all(v_cache, 'cp', 0, 1, tiled=True)
        return decode_local(x_tok, positions, keys_old, vals_old, norm_gain, w_q, b_q, w_k, b_k, w_v, b_v, w_o)

    return jax.shard_map(per_device, mesh=mesh, in_specs=(batch_spec, P('dp'), seq_spec, seq_spec, whole, whole, whole, whole, whole, whole, whole, whole), out_specs=(batch_spec, batch_spec, batch_spec), check_vma=False)
```

profile of v0, /device:TPU:113, one launch (start us, length us, event | category | flops | bytes accessed | tf_op | source)
XLA Modules:
  0.0 139.3 jit_solution(8421733984863515327)
XLA Ops:
  0.7 6.2 %all-to-all-start = ((bf16[64,64,4,128]{3,2,1,0:T(4,128)(2,1)}), bf16[64,64,4,128]{3,2,1,0:T(4,128)(2,1)}, u32[]{:S(2)}, u32[]{:S(2)}) async-start(bf16[64,64,4,128]{3,2,1,0:T(4,128)(2,1)} %param.14), calls=%async_computation | async-start | bytes 8388608 | tf_op jit(solution)/shard_map/all_to_all | solution.py:67
  6.9 0.1 fusion.25
  7.0 48.4 %all-to-all-done = bf16[64,64,4,128]{3,2,1,0:T(4,128)(2,1)} async-done(((bf16[64,64,4,128]{3,2,1,0:T(4,128)(2,1)}), bf16[64,64,4,128]{3,2,1,0:T(4,128)(2,1)}, u32[]{:S(2)}, u32[]{:S(2)}) %all-to-all-start) | async-done | bytes 4194336 | tf_op jit(solution)/shard_map/all_to_all | solution.py:67
  55.4 5.5 %all-to-all-start.1 = ((bf16[64,64,4,128]{3,2,1,0:T(4,128)(2,1)}), bf16[64,64,4,128]{3,2,1,0:T(4,128)(2,1)}, u32[]{:S(2)}, u32[]{:S(2)}) async-start(bf16[64,64,4,128]{3,2,1,0:T(4,128)(2,1)} %param.15), calls=%async_computation.1 | async-start | bytes 8388608 | tf_op jit(solution)/shard_map/all_to_all | solution.py:68
  60.9 2.7 %fusion.20 = bf16[8,4,128]{2,0,1:T(8,128)(2,1)S(1)} fusion(bf16[3584,512]{1,0:T(8,128)(2,1)} %param.21, f32[512]{0:T(512)S(1)} %convert_element_type.59, bf16[8,3584]{1,0:T(8,128)(2,1)S(1)} %copy-done.3, f32[3584]{0:T(1024)S(1)} %convert_element_type.53, f32[8]{0:T(128)S(1)} %add_rsqrt_fusion), kind=kOutput, calls=%fused_computation.18 | convolution fusion | flops 29483008 | bytes 3751968 | tf_op jit(solution)/shard_map/dot_general | solution.py:31
  63.6 0.1 fusion.35
  63.7 0.1 multiply_cosine_fusion
  63.8 2.7 %fusion.18 = f32[8,4,128]{2,0,1:T(8,128)S(1)} fusion(bf16[3584,512]{1,0:T(8,128)(2,1)} %param.19, f32[512]{0:T(512)S(1)} %convert_element_type.57, bf16[8,3584]{1,0:T(8,128)(2,1)S(1)} %copy-done.3, f32[3584]{0:T(1024)S(1)} %convert_element_type.53, f32[8]{0:T(128)S(1)} %add_rsqrt_fusion), kind=kOutput, calls=%fused_computation.16 | convolution fusion | flops 29478912 | bytes 3760160 | tf_op jit(solution)/shard_map/dot_general | solution.py:29
  66.5 0.1 subtract_convert_fusion.1
  66.6 0.1 pad_maximum_fusion
  66.7 10.1 %fusion.11 = f32[8,28,128]{2,0,1:T(8,128)S(1)} fusion(bf16[3584,3584]{1,0:T(8,128)(2,1)} %param.17, f32[3584]{0:T(1024)S(1)} %convert_element_type.55, bf16[8,3584]{1,0:T(8,128)(2,1)S(1)} %copy-done.3, f32[3584]{0:T(1024)S(1)} %convert_element_type.53, f32[8]{0:T(128)S(1)} %add_rsqrt_fusion), kind=kOutput, calls=%fused_computation.11 | convolution fusion | flops 205664256 | bytes 25890848 | tf_op jit(solution)/shard_map/dot_general | solution.py:27
  76.8 0.1 subtract_convert_fusion
  77.0 0.1 iota_compare_fusion.2
  77.1 7.3 %copy.25 = bf16[8,8,64,4,128]{4,3,2,0,1:T(4,128)(2,1)} copy(bf16[8,8,64,4,128]{4,3,2,1,0:T(4,128)(2,1)} %bitcast.3) | data formatting | bytes 8388608 | tf_op jit(solution)/shard_map/all_to_all | solution.py:67
  84.4 25.2 %all-to-all-done.1 = bf16[64,64,4,128]{3,2,1,0:T(4,128)(2,1)} async-done(((bf16[64,64,4,128]{3,2,1,0:T(4,128)(2,1)}), bf16[64,64,4,128]{3,2,1,0:T(4,128)(2,1)}, u32[]{:S(2)}, u32[]{:S(2)}) %all-to-all-start.1) | async-done | bytes 4194336 | tf_op jit(solution)/shard_map/all_to_all | solution.py:68
  109.6 4.1 %copy.28 = bf16[8,8,64,4,128]{4,3,2,0,1:T(4,128)(2,1)S(1)} copy(bf16[8,8,64,4,128]{4,3,2,1,0:T(4,128)(2,1)} %bitcast.7) | data formatting | bytes 8388608 | tf_op jit(solution)/shard_map/all_to_all | solution.py:68
  113.7 10.2 %select_select_fusion.1 = (bf16[8,512,4,128]{3,2,1,0:T(4,128)(2,1)S(1)}, bf16[8,512,4,128]{3,2,1,0:T(4,128)(2,1)S(1)}) fusion(bf16[8,512,4,128]{3,2,1,0:T(4,128)(2,1)S(1)} %bitcast.21, pred[8,512]{1,0:T(8,128)(4,1)S(1)} %get-tuple-element.14, pred[8,512]{1,0:T(8,128)(4,1)S(1)} %get-tuple-element.15, bf16[8,4,128]{2,1,0:T(4,128)(2,1)S(1)} %copy.26, ...), kind=kLoop, calls=%fused_computation.8 | loop fusion | flops 8388608 | bytes 16801792 | tf_op jit(solution)/shard_map/jit(_where)/select_n | solution.py:44
  124.0 0.0 copy-start
  124.0 2.0 %copy-done = bf16[8,512,4,128]{3,2,1,0:T(4,128)(2,1)} copy-done((bf16[8,512,4,128]{3,2,1,0:T(4,128)(2,1)}, bf16[8,512,4,128]{3,2,1,0:T(4,128)(2,1)S(1)}, u32[]{:S(2)}) %copy-start) | copy-done | bytes 4194328
  126.0 1.4 fusion.36
  127.4 0.3 fusion.21
  127.6 0.7 fusion.15
  128.4 0.1 convert_element_type.63
  128.5 10.8 %fusion = bf16[8,3584]{1,0:T(8,128)(2,1)} fusion(bf16[8,3584]{1,0:T(8,128)(2,1)S(1)} %convert_element_type.63, bf16[3584,3584]{1,0:T(8,128)(2,1)} %param.23, bf16[8,3584]{1,0:T(8,128)(2,1)S(1)} %copy-done.3), kind=kOutput, calls=%fused_computation.2 | convolution fusion | flops 205606912 | bytes 25862144 | tf_op jit(solution)/shard_map/dot_general | solution.py:54
  (26 shorter events, 0.1 us)
Async XLA Ops:
  0.6 6.2 %copy-start.6 = (bf16[512]{0:T(512)(128)(2,1)S(1)}, bf16[512]{0:T(512)(128)(2,1)}, u32[]{:S(2)}) copy-start(bf16[512]{0:T(512)(128)(2,1)} %param.22) | copy-start | bytes 3076
  0.6 6.2 %copy-start.4 = (bf16[3584]{0:T(1024)(128)(2,1)S(1)}, bf16[3584]{0:T(1024)(128)(2,1)}, u32[]{:S(2)}) copy-start(bf16[3584]{0:T(1024)(128)(2,1)} %param.16) | copy-start | bytes 21508
  0.7 6.2 %copy-start.3 = (bf16[8,3584]{1,0:T(8,128)(2,1)S(1)}, bf16[8,3584]{1,0:T(8,128)(2,1)}, u32[]{:S(2)}) copy-start(bf16[8,3584]{1,0:T(8,128)(2,1)} %param.12) | copy-start | bytes 172036
  0.7 54.7 %all-to-all-start = ((bf16[64,64,4,128]{3,2,1,0:T(4,128)(2,1)}), bf16[64,64,4,128]{3,2,1,0:T(4,128)(2,1)}, u32[]{:S(2)}, u32[]{:S(2)}) async-start(bf16[64,64,4,128]{3,2,1,0:T(4,128)(2,1)} %param.14), calls=%async_computation | async-start | bytes 8388608 | tf_op jit(solution)/shard_map/all_to_all | solution.py:67
  7.0 56.6 %copy-start.7 = (bf16[512]{0:T(512)(128)(2,1)S(1)}, bf16[512]{0:T(512)(128)(2,1)}, u32[]{:S(2)}) copy-start(bf16[512]{0:T(512)(128)(2,1)} %param.20) | copy-start | bytes 3076
  7.0 56.6 %copy-start.8 = (s32[64]{0:T(128)S(1)}, s32[64]{0:T(128)}, u32[]{:S(2)}) copy-start(s32[64]{0:T(128)} %param.13) | copy-start | bytes 772
  55.4 54.2 %all-to-all-start.1 = ((bf16[64,64,4,128]{3,2,1,0:T(4,128)(2,1)}), bf16[64,64,4,128]{3,2,1,0:T(4,128)(2,1)}, u32[]{:S(2)}, u32[]{:S(2)}) async-start(bf16[64,64,4,128]{3,2,1,0:T(4,128)(2,1)} %param.15), calls=%async_computation.1 | async-start | bytes 8388608 | tf_op jit(solution)/shard_map/all_to_all | solution.py:68
  60.9 5.7 %copy-start.5 = (bf16[3584]{0:T(1024)(128)(2,1)S(1)}, bf16[3584]{0:T(1024)(128)(2,1)}, u32[]{:S(2)}) copy-start(bf16[3584]{0:T(1024)(128)(2,1)} %param.18) | copy-start | bytes 21508
  109.6 4.1 %copy-start.1 = (bf16[8,8,64,4,128]{4,3,2,0,1:T(4,128)(2,1)S(1)}, bf16[8,8,64,4,128]{4,3,2,0,1:T(4,128)(2,1)}, u32[]{:S(2)}) copy-start(bf16[8,8,64,4,128]{4,3,2,0,1:T(4,128)(2,1)} %copy.25) | copy-start | bytes 12582916
  124.0 2.0 %copy-start = (bf16[8,512,4,128]{3,2,1,0:T(4,128)(2,1)}, bf16[8,512,4,128]{3,2,1,0:T(4,128)(2,1)S(1)}, u32[]{:S(2)}) copy-start(bf16[8,512,4,128]{3,2,1,0:T(4,128)(2,1)S(1)} %get-tuple-element.9) | copy-start | bytes 12582916
  124.0 3.6 %copy-start.2 = (bf16[8,512,4,128]{3,2,1,0:T(4,128)(2,1)}, bf16[8,512,4,128]{3,2,1,0:T(4,128)(2,1)S(1)}, u32[]{:S(2)}) copy-start(bf16[8,512,4,128]{3,2,1,0:T(4,128)(2,1)S(1)} %get-tuple-element.10) | copy-start | bytes 12582916
where the time goes:
time: 140 us; the launch traced here: 139 us
  waiting for transfers between devices  73.6 us (53%)
  matrix products  28.3 us (20%)
  local copies, waits for them, and re-layouts  13.6 us (10%)
  starting transfers between devices  11.7 us (8%)
  other arithmetic  11.2 us (8%)
    all_to_all x1, waiting for transfers between devices, per_device(): keys_old = lax.all_to_all(k_cache, 'cp', 0, 1, tiled=True)  48.4 us
    all_to_all x1, waiting for transfers between devices, per_device(): vals_old = lax.all_to_all(v_cache, 'cp', 0, 1, tiled=True)  25.2 us
    dot_general x1, matrix products, decode_local(): jnp.dot(attended, w_o, preferred_element_type=jnp.float32)  10.8 us
    select_n x1, other arithmetic, decode_local(): jnp.where(slot_idx < pos_col, keys_old, jnp.where(slot_idx == pos_col, ke...  10.2 us
    dot_general x1, matrix products, project(): jnp.dot(normed, w_q, preferred_element_type=jnp.float32)  10.1 us
    all_to_all x1, local copies, waits for them, and re-layouts, per_device(): keys_old = lax.all_to_all(k_cache, 'cp', 0, 1, tiled=True)  7.31 us
    all_to_all x1, starting transfers between devices, per_device(): keys_old = lax.all_to_all(k_cache, 'cp', 0, 1, tiled=True)  6.16 us
    all_to_all x1, starting transfers between devices, per_device(): vals_old = lax.all_to_all(v_cache, 'cp', 0, 1, tiled=True)  5.53 us
  transfers between devices with their start and end apart: 2, of which 2 were waited for; matrix products, arithmetic and copies ran while one was open for 17% of the time, Pallas kernels for 0%

commit v1 on v0

v1 whole, which is shorter than its diff:
```python
import functools

import jax
import jax.numpy as jnp
from jax import lax
from jax.experimental import pallas as pl
from jax.experimental.pallas import tpu as pltpu
from jax.sharding import PartitionSpec as P

RMS_EPS = 1e-6
ROPE_THETA = 1000000.0
PACK = 16
NEG = -1e30


def gather_kernel(n, kv_heads, lens_hbm, x_hbm, rot_hbm, gain_hbm, wq_hbm, bq_hbm, wk_hbm, bk_hbm, wv_hbm, bv_hbm, wo_hbm, k_hbm, v_hbm,
                  kbuf, vbuf, wo_ref, att_ref,
                  lens, x_ref, rot_ref, gain_ref, bq_ref, bk_ref, bv_ref, wbuf, h_ref, qf_ref, knew_ref, vnew_ref, s_ref, p_ref, acc_ref, sum_ref,
                  small_sem, wsem, wo_sem, local_sem, send_sem, recv_sem):
    rows, d_model = x_ref.shape
    head = acc_ref.shape[-1]
    q_rows = acc_ref.shape[1]
    heads = att_ref.shape[1] // head
    group = heads // kv_heads
    tiles = k_hbm.shape[1]
    block_rows = tiles * PACK
    slots = block_rows // kv_heads
    cols = wbuf.shape[2]
    me = lax.axis_index('cp')

    smalls = [
        pltpu.make_async_copy(src, dst, small_sem.at[i])
        for i, (src, dst) in enumerate([
            (lens_hbm, lens), (x_hbm, x_ref), (rot_hbm, rot_ref), (gain_hbm, gain_ref), (bq_hbm, bq_ref), (bk_hbm, bk_ref), (bv_hbm, bv_ref)])
    ]
    for copy in smalls:
        copy.start()

    blocks = [(wk_hbm, 0), (wv_hbm, 0)] + [(wq_hbm, c) for c in range(wq_hbm.shape[1] // cols)]

    def weight_copy(t):
        src, c = blocks[t]
        return pltpu.make_async_copy(src.at[:, pl.ds(c * cols, cols)], wbuf.at[t % wbuf.shape[0]], wsem.at[t % wbuf.shape[0]])

    for t in range(wbuf.shape[0]):
        weight_copy(t).start()

    def block_of(ref, owner):
        return ref.at[pl.ds(owner * rows, rows)]

    def place_of(ref, sender):
        return ref.at[:, pl.ds(sender * tiles, tiles)]

    own_k = pltpu.make_async_copy(block_of(k_hbm, me), place_of(kbuf, me), local_sem.at[0])
    own_v = pltpu.make_async_copy(block_of(v_hbm, me), place_of(vbuf, me), local_sem.at[1])
    own_k.start()
    own_v.start()

    barrier = pltpu.get_barrier_semaphore()
    peers = [lax.rem(me + k, n) for k in range(1, n)]
    for peer in peers:
        pl.semaphore_signal(barrier, inc=1, device_id={'cp': peer}, device_id_type=pl.DeviceIdType.MESH)
    pl.semaphore_wait(barrier, n - 1)

    chip, core = me // 2, lax.rem(me, 2)
    chips = n // 2

    def device(far, other):
        return lax.rem(chip + far, chips) * 2 + (core + other) % 2

    order = [(0, 1)]
    fars = sorted(range(1, chips), key=lambda f: -min(f, chips - f))
    for far in fars:
        order += [(far, 0), (far, 1)]

    def remote(which, src, dst, to):
        return pltpu.make_async_remote_copy(
            src_ref=block_of(src, to), dst_ref=place_of(dst, me),
            send_sem=send_sem.at[which, to], recv_sem=recv_sem.at[which, me],
            device_id={'cp': to}, device_id_type=pl.DeviceIdType.MESH)

    def arrival(which, src, dst, sender):
        return pltpu.make_async_remote_copy(
            src_ref=block_of(src, sender), dst_ref=place_of(dst, sender),
            send_sem=send_sem.at[which, sender], recv_sem=recv_sem.at[which, sender],
            device_id={'cp': sender}, device_id_type=pl.DeviceIdType.MESH)

    sends = []
    for which, (src, dst) in enumerate([(k_hbm, kbuf), (v_hbm, vbuf)]):
        for far, other in order:
            copy = remote(which, src, dst, device(far, other))
            copy.start()
            sends.append(copy)

    for copy in smalls:
        copy.wait()
    x_wide = x_ref[...].astype(jnp.float32)
    mean_sq = jnp.mean(x_wide * x_wide, axis=-1, keepdims=True)
    h_ref[...] = (x_wide * lax.rsqrt(mean_sq + RMS_EPS) * gain_ref[...].astype(jnp.float32)).astype(jnp.bfloat16)
    cos_t = rot_ref[0]
    sin_t = rot_ref[1]

    def rotate(v):
        return v * cos_t + pltpu.roll(v, head // 2, 1) * sin_t

    qf_ref[...] = jnp.zeros_like(qf_ref)
    for t in range(len(blocks)):
        weight_copy(t).wait()
        out = jnp.dot(h_ref[...], wbuf[t % wbuf.shape[0]], preferred_element_type=jnp.float32)
        if t + wbuf.shape[0] < len(blocks):
            weight_copy(t + wbuf.shape[0]).start()
        c = blocks[t][1]
        bias = (bk_ref if t == 0 else bv_ref if t == 1 else bq_ref)[:, c * cols:(c + 1) * cols]
        out = out + bias.astype(jnp.float32)
        for i in range(cols // head):
            part = out[:, i * head:(i + 1) * head]
            if t == 0:
                part = rotate(part).astype(jnp.bfloat16).astype(jnp.float32)
                for r in range(PACK // kv_heads):
                    knew_ref[:, r * kv_heads + i, :] = part
            elif t == 1:
                part = part.astype(jnp.bfloat16).astype(jnp.float32)
                for r in range(PACK // kv_heads):
                    vnew_ref[:, r * kv_heads + i, :] = part
            else:
                qf_ref[:, c * (cols // head) + i, :] = rotate(part)
    wo_copy = pltpu.make_async_copy(wo_hbm, wo_ref, wo_sem)
    wo_copy.start()

    def merged(s, sender, buf, new_ref):
        pos = lens[0, me * rows + s]
        tile = buf[s, pl.ds(sender * tiles, tiles)].astype(jnp.float32)
        shape = (tiles, PACK, head)
        slot = sender * slots + lax.broadcasted_iota(jnp.int32, shape, 0) * (PACK // kv_heads) + lax.broadcasted_iota(jnp.int32, shape, 1) // kv_heads
        new = jnp.broadcast_to(new_ref[s][None], shape)
        tile = jnp.where(slot < pos, tile, jnp.where(slot == pos, new, 0.0)).astype(jnp.bfloat16)
        buf[s, pl.ds(sender * tiles, tiles)] = tile
        return tile.reshape(block_rows, head)

    def keys_step(s, sender):
        pos = lens[0, me * rows + s]
        keys = merged(s, sender, kbuf, knew_ref)
        query = qf_ref[s].astype(jnp.bfloat16)
        scores = lax.dot_general(query, keys, (((1,), (1,)), ((), ())), preferred_element_type=jnp.float32) * (head ** -0.5)
        row = lax.broadcasted_iota(jnp.int32, scores.shape, 0)
        col = lax.broadcasted_iota(jnp.int32, scores.shape, 1)
        valid = (col % kv_heads == row // group) & (sender * slots + col // kv_heads <= pos)
        s_ref[s, sender] = jnp.where(valid, scores, NEG)

    def soften(s):
        scores = s_ref[s]
        top = jnp.max(jnp.max(scores, axis=0), axis=-1, keepdims=True)
        weights = jnp.exp(scores - top[None])
        sum_ref[s] = jnp.broadcast_to(jnp.sum(jnp.sum(weights, axis=0), axis=-1, keepdims=True), (q_rows, head))
        p_ref[s] = weights.astype(jnp.bfloat16)

    def values_step(s, sender):
        values = merged(s, sender, vbuf, vnew_ref)
        acc_ref[s] += jnp.dot(p_ref[s, sender], values, preferred_element_type=jnp.float32)

    def each(step):
        def body(s, carry):
            step(s)
            return carry
        lax.fori_loop(0, rows, body, 0)

    own_k.wait()
    each(lambda s: keys_step(s, me))
    for far, other in order:
        sender = device(chips - far if far else 0, other)
        arrival(0, k_hbm, kbuf, sender).wait_recv()
        each(lambda s: keys_step(s, sender))
    each(soften)
    acc_ref[...] = jnp.zeros_like(acc_ref)
    own_v.wait()
    each(lambda s: values_step(s, me))
    wo_copy.wait()
    for far, other in order:
        sender = device(chips - far if far else 0, other)
        arrival(1, v_hbm, vbuf, sender).wait_recv()
        each(lambda s: values_step(s, sender))

    for j in range(heads):
        att_ref[:, j * head:(j + 1) * head] = (acc_ref[:, j, :] / sum_ref[:, j, :]).astype(jnp.bfloat16)
    for copy in sends:
        copy.wait_send()


def finish_kernel(kbuf, vbuf, wo_ref, att_ref, x_ref, y_ref, k_out, v_out, sem):
    rows = kbuf.shape[0]
    copies = [
        pltpu.make_async_copy(src.at[b], dst.at[b], sem.at[i, b])
        for i, (src, dst) in enumerate([(kbuf, k_out), (vbuf, v_out)]) for b in range(rows)
    ]
    for copy in copies:
        copy.start()
    cols = 512
    for c in range(y_ref.shape[1] // cols):
        span = slice(c * cols, (c + 1) * cols)
        out = jnp.dot(att_ref[...], wo_ref[:, span], preferred_element_type=jnp.float32)
        y_ref[:, span] = (x_ref[:, span].astype(jnp.float32) + out).astype(jnp.bfloat16)
    for copy in copies:
        copy.wait()


def solution(mesh):
    n = mesh.shape['cp']
    batch_spec = P(('dp', 'cp'))
    seq_spec = P('dp', 'cp')
    whole = P()
    hbm = pl.BlockSpec(memory_space=pl.ANY)
    vmem = pl.BlockSpec(memory_space=pltpu.VMEM)

    def per_device(x_tok, prompt_lens, k_cache, v_cache, norm_gain, w_q, b_q, w_k, b_k, w_v, b_v, w_o):
        rows, d_model = x_tok.shape
        batch, slots, kv_heads, head = k_cache.shape
        q_cols = w_q.shape[1]
        heads = q_cols // head
        q_rows = -(-heads // PACK) * PACK
        tiles = slots * kv_heads // PACK
        all_tiles = tiles * n
        block_rows = tiles * PACK
        cols = w_k.shape[1]
        half = head // 2
        positions = lax.dynamic_slice_in_dim(prompt_lens, lax.axis_index('cp') * rows, rows)
        inv_freq = jnp.power(ROPE_THETA, -(jnp.arange(half, dtype=jnp.float32) * 2.0 / head))
        angle = positions.astype(jnp.float32)[:, None] * inv_freq
        cos_t, sin_t = jnp.cos(angle), jnp.sin(angle)
        rot = jnp.stack([jnp.concatenate([cos_t, cos_t], -1), jnp.concatenate([-sin_t, sin_t], -1)])

        bf16, f32 = jnp.bfloat16, jnp.float32
        kbuf, vbuf, wo, att = pl.pallas_call(
            functools.partial(gather_kernel, n, kv_heads),
            out_shape=[
                pltpu.VMEM((rows, all_tiles, PACK, head), bf16),
                pltpu.VMEM((rows, all_tiles, PACK, head), bf16),
                pltpu.VMEM(w_o.shape, bf16),
                pltpu.VMEM((rows, q_cols), bf16),
            ],
            in_specs=[hbm] * 13,
            out_specs=[vmem] * 4,
            scratch_shapes=[
                pltpu.SMEM((1, batch), jnp.int32),
                pltpu.VMEM((rows, d_model), bf16),
                pltpu.VMEM((2, rows, head), f32),
                pltpu.VMEM((1, d_model), bf16),
                pltpu.VMEM((1, q_cols), bf16),
                pltpu.VMEM((1, cols), bf16),
                pltpu.VMEM((1, cols), bf16),
                pltpu.VMEM((3, d_model, cols), bf16),
                pltpu.VMEM((rows, d_model), bf16),
                pltpu.VMEM((rows, q_rows, head), f32),
                pltpu.VMEM((rows, PACK, head), f32),
                pltpu.VMEM((rows, PACK, head), f32),
                pltpu.VMEM((rows, n, q_rows, block_rows), f32),
                pltpu.VMEM((rows, n, q_rows, block_rows), bf16),
                pltpu.VMEM((rows, q_rows, head), f32),
                pltpu.VMEM((rows, q_rows, head), f32),
                pltpu.SemaphoreType.DMA((7,)),
                pltpu.SemaphoreType.DMA((3,)),
                pltpu.SemaphoreType.DMA,
                pltpu.SemaphoreType.DMA((2,)),
                pltpu.SemaphoreType.DMA((2, n)),
                pltpu.SemaphoreType.DMA((2, n)),
            ],
            compiler_params=pltpu.CompilerParams(collective_id=0, has_side_effects=True, vmem_limit_bytes=28 * 1024 * 1024),
            name='gather_attend',
        )(prompt_lens[None], x_tok, rot, norm_gain[None], w_q, b_q[None], w_k, b_k[None], w_v, b_v[None], w_o,
          k_cache.reshape(batch, tiles, PACK, head), v_cache.reshape(batch, tiles, PACK, head))

        y_out, k_out, v_out = pl.pallas_call(
            finish_kernel,
            out_shape=[
                jax.ShapeDtypeStruct(x_tok.shape, bf16),
                jax.ShapeDtypeStruct(kbuf.shape, bf16),
                jax.ShapeDtypeStruct(vbuf.shape, bf16),
            ],
            in_specs=[vmem] * 5,
            out_specs=[vmem, hbm, hbm],
            scratch_shapes=[pltpu.SemaphoreType.DMA((2, rows))],
            compiler_params=pltpu.CompilerParams(vmem_limit_bytes=28 * 1024 * 1024),
            name='finish',
        )(*[pltpu.with_memory_space_constraint(a, pltpu.VMEM) for a in (kbuf, vbuf, wo, att)], x_tok)
        shape = (rows, slots * n, kv_heads, head)
        return y_out, k_out.reshape(shape), v_out.reshape(shape)

    return jax.shard_map(per_device, mesh=mesh, in_specs=(batch_spec, P('dp'), seq_spec, seq_spec, whole, whole, whole, whole, whole, whole, whole, whole), out_specs=(batch_spec, batch_spec, batch_spec), check_vma=False)
```

time: 140 us -> 115 us (0.82)
  Pallas kernels: 0 us -> 107 us
  waiting for transfers between devices: 73.6 us -> 0 us
  matrix products: 28.3 us -> 0 us
  starting transfers between devices: 11.7 us -> 0 us
  other arithmetic: 11.2 us -> 1.54 us
  local copies, waits for them, and re-layouts: 13.6 us -> 5.11 us
    pallas_call x0 -> x2, Pallas kernels: none -> 107 us  [the longest x1 99.9 us: per_device(): pl.pallas_call(functools.partial(gather_kernel, n, kv_heads), out_shape=[...]
    all_to_all x2 -> x0, waiting for transfers between devices: 73.6 us -> none  [the longest x1 48.4 us: per_device(): keys_old = lax.all_to_all(k_cache, 'cp', 0, 1, tiled=True)]
    dot_general x6 -> x0, matrix products: 28.3 us -> none  [the longest x1 10.8 us: decode_local(): jnp.dot(attended, w_o, preferred_element_type=jnp.float32)]
    all_to_all x2 -> x0, starting transfers between devices: 11.7 us -> none  [the longest x1 6.16 us: per_device(): keys_old = lax.all_to_all(k_cache, 'cp', 0, 1, tiled=True)]
    all_to_all x2 -> x0, local copies, waits for them, and re-layouts: 11.4 us -> none  [the longest x1 7.31 us: per_device(): keys_old = lax.all_to_all(k_cache, 'cp', 0, 1, tiled=True)]
    select_n x1 -> x0, other arithmetic: 10.2 us -> none  [decode_local(): jnp.where(slot_idx < pos_col, keys_old, jnp.where(slot_idx == pos_col, ke...]
    broadcast_in_dim x0 -> x4, local copies, waits for them, and re-layouts: none -> 5.11 us  [the longest x1 1.3 us: per_device(): norm_gain[None]]
    unnamed x18 -> x0, local copies, waits for them, and re-layouts: 2.03 us -> none
  transfers between devices with their start and end apart: 2 -> 0, of which waited for: 2 -> 0; matrix products, arithmetic and copies ran while one was open for 17% -> 0% of each run, Pallas kernels for 0% -> 0%
where the time goes in v1:
time: 115 us
  Pallas kernels  107 us (93%)
  local copies, waits for them, and re-layouts  5.11 us (4%)
  other arithmetic  1.54 us (1%)
    pallas_call x1, Pallas kernels, per_device(): pl.pallas_call(functools.partial(gather_kernel, n, kv_heads), out_shape=[...  99.9 us
    pallas_call x1, Pallas kernels, per_device(): pl.pallas_call(finish_kernel, out_shape=[jax.ShapeDtypeStruct(x_tok.shape...  7.59 us

profile of v1, /device:TPU:113, one launch (start us, length us, event | category | flops | bytes accessed | tf_op | source)
XLA Modules:
  0.0 114.8 jit_solution(7635906145914545509)
XLA Ops:
  0.6 0.7 dynamic-slice_convert_fusion
  1.4 1.2 %broadcast_in_dim.20.bk_hbm = bf16[1,512]{1,0:T(2,128)(2,1)} reshape(bf16[512]{0:T(512)(128)(2,1)} %param.20) | data formatting | bytes 2048 | tf_op jit(solution)/shard_map/broadcast_in_dim | solution.py:268
  2.6 1.3 %broadcast_in_dim.21.bv_hbm = bf16[1,512]{1,0:T(2,128)(2,1)} reshape(bf16[512]{0:T(512)(128)(2,1)} %param.22) | data formatting | bytes 2048 | tf_op jit(solution)/shard_map/broadcast_in_dim | solution.py:268
  3.9 0.1 multiply_cosine_fusion
  4.0 0.1 maximum_bitcast_fusion
  4.1 0.6 pad_maximum_fusion.rot_hbm
  4.7 1.3 %broadcast_in_dim.18.gain_hbm = bf16[1,3584]{1,0:T(2,128)(2,1)} reshape(bf16[3584]{0:T(1024)(128)(2,1)} %param.16) | data formatting | bytes 14336 | tf_op jit(solution)/shard_map/broadcast_in_dim | solution.py:268
  6.0 1.3 %broadcast_in_dim.19.bq_hbm = bf16[1,3584]{1,0:T(2,128)(2,1)} reshape(bf16[3584]{0:T(1024)(128)(2,1)} %param.18) | data formatting | bytes 14336 | tf_op jit(solution)/shard_map/broadcast_in_dim | solution.py:268
  7.3 99.9 %gather_attend.1 = (bf16[8,128,16,128]{3,2,1,0:T(8,128)(2,1)S(1)}, bf16[8,128,16,128]{3,2,1,0:T(8,128)(2,1)S(1)}, bf16[3584,3584]{1,0:T(8,128)(2,1)S(1)}, bf16[8,3584]{1,0:T(8,128)(2,1)S(1)}) custom-call(s32[1,64]{1,0:T(1,128)} %bitcast.11, bf16[8,3584]{1,0:T(8,128)(2,1)} %x_ref.1, f32[2,8,128]{2,1,0:T(8,128)} %pad_maximum_fusion.rot_hbm, ...), custom_call_target="tpu_custom_call" | custom-call | tf_op jit(solution)/shard_map/gather_attend/pallas_call | solution.py:232
  107.2 7.6 %finish.1 = (bf16[8,3584]{1,0:T(8,128)(2,1)}, bf16[8,128,16,128]{3,2,1,0:T(8,128)(2,1)}, bf16[8,128,16,128]{3,2,1,0:T(8,128)(2,1)}) custom-call(bf16[8,128,16,128]{3,2,1,0:T(8,128)(2,1)S(1)} %get-tuple-element.10.kbuf, bf16[8,128,16,128]{3,2,1,0:T(8,128)(2,1)S(1)} %get-tuple-element.11.vbuf, bf16[3584,3584]{1,0:T(8,128)(2,1)S(1)} %get-tuple-element.12.wo_ref, ...), custom_call_target="tpu_custom_call" | custom-call | tf_op jit(solution)/shard_map/finish/pallas_call | solution.py:271
  (1 shorter events, 0.0 us)

commit v2 on v1

v2 whole, which is shorter than its diff:
```python
import functools

import jax
import jax.numpy as jnp
import numpy as np
from jax import lax
from jax.experimental import pallas as pl
from jax.experimental.pallas import tpu as pltpu
from jax.sharding import PartitionSpec as P

RMS_EPS = 1e-6
ROPE_THETA = 1000000.0
PACK = 16
NEG = -1e30


def gather_kernel(n, kv_heads, lens_hbm, x_hbm, freq_hbm, gain_hbm, wq_hbm, bq_hbm, wk_hbm, bk_hbm, wv_hbm, bv_hbm, wo_hbm, k_hbm, v_hbm,
                  kbuf, vbuf, wo_ref, att_ref,
                  lens, x_ref, freq_ref, gain_ref, bq_ref, bk_ref, bv_ref, wbuf, h_ref, qf_ref, knew_ref, vnew_ref, s_ref, p_ref, acc_ref, sum_ref,
                  small_sem, wsem, wo_sem, k_send, k_recv, v_send, v_recv):
    rows, d_model = x_ref.shape
    head = acc_ref.shape[-1]
    q_rows = acc_ref.shape[1]
    heads = att_ref.shape[1] // head
    group = heads // kv_heads
    tiles = k_hbm.shape[1]
    block_rows = tiles * PACK
    slots = block_rows // kv_heads
    cols = wbuf.shape[2]
    me = lax.axis_index('cp')

    chip, core = me // 2, lax.rem(me, 2)
    chips = n // 2
    parts = v_recv.shape[1]
    part_rows = rows // parts

    fars = sorted(range(1, chips), key=lambda f: -min(f, chips - f))

    def place(t, way):
        far = sum(jnp.where(t // 2 == k + 1, f, 0) for k, f in enumerate(fars))
        return lax.rem(chip + way * far + chips, chips) * 2 + lax.rem(core + t, 2)

    def block(ref, owner, part, count):
        return ref.at[pl.ds(owner * rows + part * count, count)]

    def span(ref, sender, part, count):
        return ref.at[pl.ds(part * count, count), pl.ds(sender * tiles, tiles)]

    def keys_copy(to, sender):
        return pltpu.make_async_remote_copy(
            src_ref=block(k_hbm, to, 0, rows), dst_ref=span(kbuf, sender, 0, rows), send_sem=k_send.at[to], recv_sem=k_recv.at[sender],
            device_id={'cp': to}, device_id_type=pl.DeviceIdType.MESH)

    def values_copy(to, sender, part):
        return pltpu.make_async_remote_copy(
            src_ref=block(v_hbm, to, part, part_rows), dst_ref=span(vbuf, sender, part, part_rows), send_sem=v_send.at[to, part],
            recv_sem=v_recv.at[sender, part], device_id={'cp': to}, device_id_type=pl.DeviceIdType.MESH)

    barrier = pltpu.get_barrier_semaphore()
    for t in range(1, n):
        pl.semaphore_signal(barrier, inc=1, device_id={'cp': place(t, 1)}, device_id_type=pl.DeviceIdType.MESH)

    smalls = [
        pltpu.make_async_copy(src, dst, small_sem.at[i])
        for i, (src, dst) in enumerate([
            (lens_hbm, lens), (x_hbm, x_ref), (freq_hbm, freq_ref), (gain_hbm, gain_ref), (bq_hbm, bq_ref), (bk_hbm, bk_ref), (bv_hbm, bv_ref)])
    ]
    for copy in smalls:
        copy.start()

    blocks = [(wk_hbm, 0), (wv_hbm, 0)] + [(wq_hbm, c) for c in range(wq_hbm.shape[1] // cols)]

    def weight_copy(t):
        src, c = blocks[t]
        return pltpu.make_async_copy(src.at[:, pl.ds(c * cols, cols)], wbuf.at[t % wbuf.shape[0]], wsem.at[t % wbuf.shape[0]])

    for t in range(wbuf.shape[0]):
        weight_copy(t).start()

    pltpu.make_async_copy(block(k_hbm, me, 0, rows), span(kbuf, me, 0, rows), k_recv.at[me]).start()
    for part in range(parts):
        pltpu.make_async_copy(block(v_hbm, me, part, part_rows), span(vbuf, me, part, part_rows), v_recv.at[me, part]).start()

    pl.semaphore_wait(barrier, n - 1)
    for t in range(1, n):
        keys_copy(place(t, 1), me).start()
    for part in range(parts):
        for t in range(1, n):
            values_copy(place(t, 1), me, part).start()

    for copy in smalls:
        copy.wait()
    x_wide = x_ref[...].astype(jnp.float32)
    mean_sq = jnp.mean(x_wide * x_wide, axis=-1, keepdims=True)
    h_ref[...] = (x_wide * lax.rsqrt(mean_sq + RMS_EPS) * gain_ref[...].astype(jnp.float32)[None]).astype(jnp.bfloat16)
    row = lax.broadcasted_iota(jnp.int32, (rows, head), 0)
    lane = lax.broadcasted_iota(jnp.int32, (rows, head), 1)
    positions = sum(jnp.where(row == b, lens[me * rows + b], 0) for b in range(rows))
    angle = positions.astype(jnp.float32) * freq_ref[...]
    cos_t = jnp.cos(angle)
    sin_t = jnp.where(lane < head // 2, -jnp.sin(angle), jnp.sin(angle))

    def rotate(v):
        return v * cos_t + pltpu.roll(v, head // 2, 1) * sin_t

    qf_ref[...] = jnp.zeros_like(qf_ref)
    for t in range(len(blocks)):
        weight_copy(t).wait()
        out = jnp.dot(h_ref[...], wbuf[t % wbuf.shape[0]], preferred_element_type=jnp.float32)
        if t + wbuf.shape[0] < len(blocks):
            weight_copy(t + wbuf.shape[0]).start()
        c = blocks[t][1]
        bias = (bk_ref if t == 0 else bv_ref if t == 1 else bq_ref)[c * cols:(c + 1) * cols]
        out = out + bias.astype(jnp.float32)[None]
        for i in range(cols // head):
            part = out[:, i * head:(i + 1) * head]
            if t == 0:
                part = rotate(part).astype(jnp.bfloat16).astype(jnp.float32)
                for r in range(PACK // kv_heads):
                    knew_ref[:, r * kv_heads + i, :] = part
            elif t == 1:
                part = part.astype(jnp.bfloat16).astype(jnp.float32)
                for r in range(PACK // kv_heads):
                    vnew_ref[:, r * kv_heads + i, :] = part
            else:
                qf_ref[:, c * (cols // head) + i, :] = rotate(part)
    wo_copy = pltpu.make_async_copy(wo_hbm, wo_ref, wo_sem)
    wo_copy.start()

    def merged(s, sender, buf, new_ref):
        pos = lens[me * rows + s]
        tile = buf[s, pl.ds(sender * tiles, tiles)].astype(jnp.float32)
        shape = (tiles, PACK, head)
        slot = sender * slots + lax.broadcasted_iota(jnp.int32, shape, 0) * (PACK // kv_heads) + lax.broadcasted_iota(jnp.int32, shape, 1) // kv_heads
        new = jnp.broadcast_to(new_ref[s][None], shape)
        tile = jnp.where(slot < pos, tile, jnp.where(slot == pos, new, 0.0)).astype(jnp.bfloat16)
        buf[s, pl.ds(sender * tiles, tiles)] = tile
        return tile.reshape(block_rows, head)

    def keys_step(s, sender):
        pos = lens[me * rows + s]
        keys = merged(s, sender, kbuf, knew_ref)
        query = qf_ref[s].astype(jnp.bfloat16)
        scores = lax.dot_general(query, keys, (((1,), (1,)), ((), ())), preferred_element_type=jnp.float32) * (head ** -0.5)
        row = lax.broadcasted_iota(jnp.int32, scores.shape, 0)
        col = lax.broadcasted_iota(jnp.int32, scores.shape, 1)
        valid = (col % kv_heads == row // group) & (sender * slots + col // kv_heads <= pos)
        s_ref[s, sender] = jnp.where(valid, scores, NEG)
        return 0

    def soften(s):
        scores = s_ref[s]
        top = jnp.max(jnp.max(scores, axis=0), axis=-1, keepdims=True)
        weights = jnp.exp(scores - top[None])
        sum_ref[s] = jnp.broadcast_to(jnp.sum(jnp.sum(weights, axis=0), axis=-1, keepdims=True), (q_rows, head))
        p_ref[s] = weights.astype(jnp.bfloat16)
        return 0

    def values_step(s, sender):
        values = merged(s, sender, vbuf, vnew_ref)
        acc_ref[s] += jnp.dot(p_ref[s, sender], values, preferred_element_type=jnp.float32)
        return 0

    def keys_arrival(t, carry):
        sender = place(t, -1)
        keys_copy(sender, sender).wait_recv()
        return lax.fori_loop(0, rows, lambda s, c: keys_step(s, sender), carry)

    def values_arrival(u, carry):
        part, sender = u // n, place(lax.rem(u, n), -1)
        values_copy(sender, sender, part).wait_recv()
        return lax.fori_loop(part * part_rows, (part + 1) * part_rows, lambda s, c: values_step(s, sender), carry)

    lax.fori_loop(0, n, keys_arrival, 0)
    lax.fori_loop(0, rows, lambda s, c: soften(s), 0)
    acc_ref[...] = jnp.zeros_like(acc_ref)
    wo_copy.wait()
    lax.fori_loop(0, n * parts, values_arrival, 0)

    for j in range(heads):
        att_ref[:, j * head:(j + 1) * head] = (acc_ref[:, j, :] / sum_ref[:, j, :]).astype(jnp.bfloat16)
    for t in range(1, n):
        keys_copy(place(t, 1), me).wait_send()
        for part in range(parts):
            values_copy(place(t, 1), me, part).wait_send()


def finish_kernel(kbuf, vbuf, wo_ref, att_ref, x_ref, y_ref, k_out, v_out, sem):
    rows = kbuf.shape[0]
    copies = [
        pltpu.make_async_copy(src.at[b], dst.at[b], sem.at[i, b])
        for i, (src, dst) in enumerate([(kbuf, k_out), (vbuf, v_out)]) for b in range(rows)
    ]
    for copy in copies:
        copy.start()
    cols = 512

    def project(c, carry):
        span = pl.ds(pl.multiple_of(c * cols, cols), cols)
        out = jnp.dot(att_ref[...], wo_ref[:, span], preferred_element_type=jnp.float32)
        y_ref[:, span] = (x_ref[:, span].astype(jnp.float32) + out).astype(jnp.bfloat16)
        return carry

    lax.fori_loop(0, y_ref.shape[1] // cols, project, 0)
    for copy in copies:
        copy.wait()


def solution(mesh):
    n = mesh.shape['cp']
    batch_spec = P(('dp', 'cp'))
    seq_spec = P('dp', 'cp')
    whole = P()
    hbm = pl.BlockSpec(memory_space=pl.ANY)
    vmem = pl.BlockSpec(memory_space=pltpu.VMEM)

    def per_device(x_tok, prompt_lens, k_cache, v_cache, norm_gain, w_q, b_q, w_k, b_k, w_v, b_v, w_o):
        rows, d_model = x_tok.shape
        batch, slots, kv_heads, head = k_cache.shape
        q_cols = w_q.shape[1]
        heads = q_cols // head
        q_rows = -(-heads // PACK) * PACK
        tiles = slots * kv_heads // PACK
        all_tiles = tiles * n
        block_rows = tiles * PACK
        cols = w_k.shape[1]
        half = head // 2
        freq = np.power(ROPE_THETA, -np.arange(half) * 2.0 / head).astype(np.float32)
        freq = jnp.asarray(np.concatenate([freq, freq])[None])
        parts = 4

        bf16, f32 = jnp.bfloat16, jnp.float32
        kbuf, vbuf, wo, att = pl.pallas_call(
            functools.partial(gather_kernel, n, kv_heads),
            out_shape=[
                pltpu.VMEM((rows, all_tiles, PACK, head), bf16),
                pltpu.VMEM((rows, all_tiles, PACK, head), bf16),
                pltpu.VMEM(w_o.shape, bf16),
                pltpu.VMEM((rows, q_cols), bf16),
            ],
            in_specs=[hbm] * 13,
            out_specs=[vmem] * 4,
            scratch_shapes=[
                pltpu.SMEM((batch,), jnp.int32),
                pltpu.VMEM((rows, d_model), bf16),
                pltpu.VMEM((1, head), f32),
                pltpu.VMEM((d_model,), bf16),
                pltpu.VMEM((q_cols,), bf16),
                pltpu.VMEM((cols,), bf16),
                pltpu.VMEM((cols,), bf16),
                pltpu.VMEM((3, d_model, cols), bf16),
                pltpu.VMEM((rows, d_model), bf16),
                pltpu.VMEM((rows, q_rows, head), f32),
                pltpu.VMEM((rows, PACK, head), f32),
                pltpu.VMEM((rows, PACK, head), f32),
                pltpu.VMEM((rows, n, q_rows, block_rows), f32),
                pltpu.VMEM((rows, n, q_rows, block_rows), bf16),
                pltpu.VMEM((rows, q_rows, head), f32),
                pltpu.VMEM((rows, q_rows, head), f32),
                pltpu.SemaphoreType.DMA((7,)),
                pltpu.SemaphoreType.DMA((3,)),
                pltpu.SemaphoreType.DMA,
                pltpu.SemaphoreType.DMA((n,)),
                pltpu.SemaphoreType.DMA((n,)),
                pltpu.SemaphoreType.DMA((n, parts)),
                pltpu.SemaphoreType.DMA((n, parts)),
            ],
            compiler_params=pltpu.CompilerParams(collective_id=0, has_side_effects=True, vmem_limit_bytes=28 * 1024 * 1024),
            name='gather_attend',
        )(prompt_lens, x_tok, freq, norm_gain, w_q, b_q, w_k, b_k, w_v, b_v, w_o,
          k_cache.reshape(batch, tiles, PACK, head), v_cache.reshape(batch, tiles, PACK, head))

        y_out, k_out, v_out = pl.pallas_call(
            finish_kernel,
            out_shape=[
                jax.ShapeDtypeStruct(x_tok.shape, bf16),
                jax.ShapeDtypeStruct(kbuf.shape, bf16),
                jax.ShapeDtypeStruct(vbuf.shape, bf16),
            ],
            in_specs=[vmem] * 5,
            out_specs=[vmem, hbm, hbm],
            scratch_shapes=[pltpu.SemaphoreType.DMA((2, rows))],
            compiler_params=pltpu.CompilerParams(vmem_limit_bytes=28 * 1024 * 1024),
            name='finish',
        )(*[pltpu.with_memory_space_constraint(a, pltpu.VMEM) for a in (kbuf, vbuf, wo, att)], x_tok)
        shape = (rows, slots * n, kv_heads, head)
        return y_out, k_out.reshape(shape), v_out.reshape(shape)

    return jax.shard_map(per_device, mesh=mesh, in_specs=(batch_spec, P('dp'), seq_spec, seq_spec, whole, whole, whole, whole, whole, whole, whole, whole), out_specs=(batch_spec, batch_spec, batch_spec), check_vma=False)
```

time: 115 us -> 104 us (0.904)
  local copies, waits for them, and re-layouts: 5.11 us -> 0 us
  Pallas kernels: 107 us -> 104 us
  other arithmetic: 1.54 us -> 0 us
    broadcast_in_dim x4 -> x0, local copies, waits for them, and re-layouts: 5.11 us -> none  [the longest x1 1.3 us: per_device(): norm_gain[None]]
    pallas_call x1, Pallas kernels: 99.9 us -> 97.8 us  [per_device(): pl.pallas_call(functools.partial(gather_kernel, n, kv_heads), out_shape=[...]
    pallas_call x1, Pallas kernels: 7.59 us -> 5.82 us  [per_device(): pl.pallas_call(finish_kernel, out_shape=[jax.ShapeDtypeStruct(x_tok.shape...]
where the time goes in v2:
time: 104 us
  Pallas kernels  104 us (100%)
    pallas_call x1, Pallas kernels, per_device(): pl.pallas_call(functools.partial(gather_kernel, n, kv_heads), out_shape=[...  97.8 us
    pallas_call x1, Pallas kernels, per_device(): pl.pallas_call(finish_kernel, out_shape=[jax.ShapeDtypeStruct(x_tok.shape...  5.82 us

profile of v2, /device:TPU:113, one launch (start us, length us, event | category | flops | bytes accessed | tf_op | source)
XLA Modules:
  0.0 104.2 jit_solution(3067745045853367806)
XLA Ops:
  0.6 97.8 %gather_attend.1 = (bf16[8,128,16,128]{3,2,1,0:T(8,128)(2,1)S(1)}, bf16[8,128,16,128]{3,2,1,0:T(8,128)(2,1)S(1)}, bf16[3584,3584]{1,0:T(8,128)(2,1)S(1)}, bf16[8,3584]{1,0:T(8,128)(2,1)S(1)}) custom-call(s32[64]{0:T(128)} %lens_hbm.1, bf16[8,3584]{1,0:T(8,128)(2,1)} %x_ref.1, f32[1,128]{1,0:T(1,128)} %constant.2.clone.freq_hbm, bf16[3584]{0:T(1024)(128)(2,1)} %gain_hbm.1, ...), custom_call_target="tpu_custom_call" | custom-call | tf_op jit(solution)/shard_map/gather_attend/pallas_call | solution.py:233
  98.4 5.8 %finish.1 = (bf16[8,3584]{1,0:T(8,128)(2,1)}, bf16[8,128,16,128]{3,2,1,0:T(8,128)(2,1)}, bf16[8,128,16,128]{3,2,1,0:T(8,128)(2,1)}) custom-call(bf16[8,128,16,128]{3,2,1,0:T(8,128)(2,1)S(1)} %get-tuple-element.10.kbuf, bf16[8,128,16,128]{3,2,1,0:T(8,128)(2,1)S(1)} %get-tuple-element.11.vbuf, bf16[3584,3584]{1,0:T(8,128)(2,1)S(1)} %get-tuple-element.12.wo_ref, ...), custom_call_target="tpu_custom_call" | custom-call | tf_op jit(solution)/shard_map/finish/pallas_call | solution.py:273

commit v3 on v2

--- a/solution.py
+++ b/solution.py
@@ -15,8 +15,8 @@
 
 
 def gather_kernel(n, kv_heads, lens_hbm, x_hbm, freq_hbm, gain_hbm, wq_hbm, bq_hbm, wk_hbm, bk_hbm, wv_hbm, bv_hbm, wo_hbm, k_hbm, v_hbm,
-                  kbuf, vbuf, wo_ref, att_ref,
-                  lens, x_ref, freq_ref, gain_ref, bq_ref, bk_ref, bv_ref, wbuf, h_ref, qf_ref, knew_ref, vnew_ref, s_ref, p_ref, acc_ref, sum_ref,
+                  kbuf, vbuf, wo_ref, att_ref, x_ref,
+                  lens, freq_ref, gain_ref, bq_ref, bk_ref, bv_ref, wbuf, h_ref, qf_ref, knew_ref, vnew_ref, s_ref, p_ref, acc_ref, sum_ref,
                   small_sem, wsem, wo_sem, k_send, k_recv, v_send, v_recv):
     rows, d_model = x_ref.shape
     head = acc_ref.shape[-1]
@@ -185,7 +185,7 @@
             values_copy(place(t, 1), me, part).wait_send()
 
 
-def finish_kernel(kbuf, vbuf, wo_ref, att_ref, x_ref, y_ref, k_out, v_out, sem):
+def finish_kernel(kbuf, vbuf, wo_ref, att_ref, x_ref, y_out, k_out, v_out, y_ref, sem, y_sem):
     rows = kbuf.shape[0]
     copies = [
         pltpu.make_async_copy(src.at[b], dst.at[b], sem.at[i, b])
@@ -202,8 +202,11 @@
         return carry
 
     lax.fori_loop(0, y_ref.shape[1] // cols, project, 0)
+    y_copy = pltpu.make_async_copy(y_ref, y_out, y_sem)
+    y_copy.start()
     for copy in copies:
         copy.wait()
+    y_copy.wait()
 
 
 def solution(mesh):
@@ -230,19 +233,19 @@
         parts = 4
 
         bf16, f32 = jnp.bfloat16, jnp.float32
-        kbuf, vbuf, wo, att = pl.pallas_call(
+        kbuf, vbuf, wo, att, x_near = pl.pallas_call(
             functools.partial(gather_kernel, n, kv_heads),
             out_shape=[
                 pltpu.VMEM((rows, all_tiles, PACK, head), bf16),
                 pltpu.VMEM((rows, all_tiles, PACK, head), bf16),
                 pltpu.VMEM(w_o.shape, bf16),
                 pltpu.VMEM((rows, q_cols), bf16),
+                pltpu.VMEM((rows, d_model), bf16),
             ],
             in_specs=[hbm] * 13,
-            out_specs=[vmem] * 4,
+            out_specs=[vmem] * 5,
             scratch_shapes=[
                 pltpu.SMEM((batch,), jnp.int32),
-                pltpu.VMEM((rows, d_model), bf16),
                 pltpu.VMEM((1, head), f32),
                 pltpu.VMEM((d_model,), bf16),
                 pltpu.VMEM((q_cols,), bf16),
@@ -278,11 +281,11 @@
                 jax.ShapeDtypeStruct(vbuf.shape, bf16),
             ],
             in_specs=[vmem] * 5,
-            out_specs=[vmem, hbm, hbm],
-            scratch_shapes=[pltpu.SemaphoreType.DMA((2, rows))],
+            out_specs=[hbm] * 3,
+            scratch_shapes=[pltpu.VMEM(x_tok.shape, bf16), pltpu.SemaphoreType.DMA((2, rows)), pltpu.SemaphoreType.DMA],
             compiler_params=pltpu.CompilerParams(vmem_limit_bytes=28 * 1024 * 1024),
             name='finish',
-        )(*[pltpu.with_memory_space_constraint(a, pltpu.VMEM) for a in (kbuf, vbuf, wo, att)], x_tok)
+        )(*[pltpu.with_memory_space_constraint(a, pltpu.VMEM) for a in (kbuf, vbuf, wo, att, x_near)])
         shape = (rows, slots * n, kv_heads, head)
         return y_out, k_out.reshape(shape), v_out.reshape(shape)
 

time: 104 us -> 103 us (level)
  no operation moved by 1% of the time
where the time goes in v3:
time: 103 us
  Pallas kernels  103 us (100%)
    pallas_call x1, Pallas kernels, per_device(): pl.pallas_call(functools.partial(gather_kernel, n, kv_heads), out_shape=[...  97.8 us
    pallas_call x1, Pallas kernels, per_device(): pl.pallas_call(finish_kernel, out_shape=[jax.ShapeDtypeStruct(x_tok.shape...  5 us

profile of v3, /device:TPU:113, one launch (start us, length us, event | category | flops | bytes accessed | tf_op | source)
XLA Modules:
  0.0 103.4 jit_solution(17282715769607030566)
XLA Ops:
  0.6 97.8 %gather_attend.1 = (bf16[8,128,16,128]{3,2,1,0:T(8,128)(2,1)S(1)}, bf16[8,128,16,128]{3,2,1,0:T(8,128)(2,1)S(1)}, bf16[3584,3584]{1,0:T(8,128)(2,1)S(1)}, bf16[8,3584]{1,0:T(8,128)(2,1)S(1)}, bf16[8,3584]{1,0:T(8,128)(2,1)S(1)}) custom-call(s32[64]{0:T(128)} %lens_hbm.1, bf16[8,3584]{1,0:T(8,128)(2,1)} %x_hbm.1, f32[1,128]{1,0:T(1,128)} %constant.2.clone.freq_hbm, ...), custom_call_target="tpu_custom_call" | custom-call | tf_op jit(solution)/shard_map/gather_attend/pallas_call | solution.py:236
  98.4 5.0 %finish.1 = (bf16[8,3584]{1,0:T(8,128)(2,1)}, bf16[8,128,16,128]{3,2,1,0:T(8,128)(2,1)}, bf16[8,128,16,128]{3,2,1,0:T(8,128)(2,1)}) custom-call(bf16[8,128,16,128]{3,2,1,0:T(8,128)(2,1)S(1)} %get-tuple-element.11.kbuf, bf16[8,128,16,128]{3,2,1,0:T(8,128)(2,1)S(1)} %get-tuple-element.12.vbuf, bf16[3584,3584]{1,0:T(8,128)(2,1)S(1)} %get-tuple-element.13.wo_ref, ...), custom_call_target="tpu_custom_call" | custom-call | tf_op jit(solution)/shard_map/finish/pallas_call | solution.py:276

commit v4 on v3

--- a/solution.py
+++ b/solution.py
@@ -16,8 +16,8 @@
 
 def gather_kernel(n, kv_heads, lens_hbm, x_hbm, freq_hbm, gain_hbm, wq_hbm, bq_hbm, wk_hbm, bk_hbm, wv_hbm, bv_hbm, wo_hbm, k_hbm, v_hbm,
                   kbuf, vbuf, wo_ref, att_ref, x_ref,
-                  lens, freq_ref, gain_ref, bq_ref, bk_ref, bv_ref, wbuf, h_ref, qf_ref, knew_ref, vnew_ref, s_ref, p_ref, acc_ref, sum_ref,
-                  small_sem, wsem, wo_sem, k_send, k_recv, v_send, v_recv):
+                  lens, freq_ref, gain_ref, bq_ref, bk_ref, bv_ref, wbuf, k_near, v_near, h_ref, qf_ref, knew_ref, vnew_ref, s_ref, p_ref, acc_ref, sum_ref,
+                  small_sem, wsem, wo_sem, near_sem, k_send, k_recv, v_send, v_recv):
     rows, d_model = x_ref.shape
     head = acc_ref.shape[-1]
     q_rows = acc_ref.shape[1]
@@ -48,17 +48,24 @@
 
     def keys_copy(to, sender):
         return pltpu.make_async_remote_copy(
-            src_ref=block(k_hbm, to, 0, rows), dst_ref=span(kbuf, sender, 0, rows), send_sem=k_send.at[to], recv_sem=k_recv.at[sender],
+            src_ref=block(k_near, to, 0, rows), dst_ref=span(kbuf, sender, 0, rows), send_sem=k_send.at[to], recv_sem=k_recv.at[sender],
             device_id={'cp': to}, device_id_type=pl.DeviceIdType.MESH)
 
     def values_copy(to, sender, part):
         return pltpu.make_async_remote_copy(
-            src_ref=block(v_hbm, to, part, part_rows), dst_ref=span(vbuf, sender, part, part_rows), send_sem=v_send.at[to, part],
+            src_ref=block(v_near, to, part, part_rows), dst_ref=span(vbuf, sender, part, part_rows), send_sem=v_send.at[to, part],
             recv_sem=v_recv.at[sender, part], device_id={'cp': to}, device_id_type=pl.DeviceIdType.MESH)
 
     barrier = pltpu.get_barrier_semaphore()
     for t in range(1, n):
         pl.semaphore_signal(barrier, inc=1, device_id={'cp': place(t, 1)}, device_id_type=pl.DeviceIdType.MESH)
+
+    def stage(which, to):
+        src, dst = ((k_hbm, k_near), (v_hbm, v_near))[which]
+        return pltpu.make_async_copy(block(src, to, 0, rows), block(dst, to, 0, rows), near_sem.at[which, to])
+
+    for t in range(1, n):
+        stage(0, place(t, 1)).start()
 
     smalls = [
         pltpu.make_async_copy(src, dst, small_sem.at[i])
@@ -74,16 +81,20 @@
         src, c = blocks[t]
         return pltpu.make_async_copy(src.at[:, pl.ds(c * cols, cols)], wbuf.at[t % wbuf.shape[0]], wsem.at[t % wbuf.shape[0]])
 
+    pltpu.make_async_copy(block(k_hbm, me, 0, rows), span(kbuf, me, 0, rows), k_recv.at[me]).start()
+    for t in range(1, n):
+        stage(1, place(t, 1)).start()
     for t in range(wbuf.shape[0]):
         weight_copy(t).start()
-
-    pltpu.make_async_copy(block(k_hbm, me, 0, rows), span(kbuf, me, 0, rows), k_recv.at[me]).start()
     for part in range(parts):
         pltpu.make_async_copy(block(v_hbm, me, part, part_rows), span(vbuf, me, part, part_rows), v_recv.at[me, part]).start()
 
     pl.semaphore_wait(barrier, n - 1)
     for t in range(1, n):
+        stage(0, place(t, 1)).wait()
         keys_copy(place(t, 1), me).start()
+    for t in range(1, n):
+        stage(1, place(t, 1)).wait()
     for part in range(parts):
         for t in range(1, n):
             values_copy(place(t, 1), me, part).start()
@@ -230,7 +241,7 @@
         half = head // 2
         freq = np.power(ROPE_THETA, -np.arange(half) * 2.0 / head).astype(np.float32)
         freq = jnp.asarray(np.concatenate([freq, freq])[None])
-        parts = 4
+        parts = rows
 
         bf16, f32 = jnp.bfloat16, jnp.float32
         kbuf, vbuf, wo, att, x_near = pl.pallas_call(
@@ -252,6 +263,8 @@
                 pltpu.VMEM((cols,), bf16),
                 pltpu.VMEM((cols,), bf16),
                 pltpu.VMEM((3, d_model, cols), bf16),
+                pltpu.VMEM((batch, tiles, PACK, head), bf16),
+                pltpu.VMEM((batch, tiles, PACK, head), bf16),
                 pltpu.VMEM((rows, d_model), bf16),
                 pltpu.VMEM((rows, q_rows, head), f32),
                 pltpu.VMEM((rows, PACK, head), f32),
@@ -263,6 +276,7 @@
                 pltpu.SemaphoreType.DMA((7,)),
                 pltpu.SemaphoreType.DMA((3,)),
                 pltpu.SemaphoreType.DMA,
+                pltpu.SemaphoreType.DMA((2, n)),
                 pltpu.SemaphoreType.DMA((n,)),
                 pltpu.SemaphoreType.DMA((n,)),
                 pltpu.SemaphoreType.DMA((n, parts)),

time: 103 us -> 104 us (level)
  no operation moved by 1% of the time
where the time goes in v4:
time: 104 us
  Pallas kernels  103 us (99%)
    pallas_call x1, Pallas kernels, per_device(): pl.pallas_call(functools.partial(gather_kernel, n, kv_heads), out_shape=[...  98.3 us
    pallas_call x1, Pallas kernels, per_device(): pl.pallas_call(finish_kernel, out_shape=[jax.ShapeDtypeStruct(x_tok.shape...  5 us

profile of v4, /device:TPU:113, one launch (start us, length us, event | category | flops | bytes accessed | tf_op | source)
XLA Modules:
  0.0 104.0 jit_solution(10667407256137549230)
XLA Ops:
  0.6 98.3 %gather_attend.1 = (bf16[8,128,16,128]{3,2,1,0:T(8,128)(2,1)S(1)}, bf16[8,128,16,128]{3,2,1,0:T(8,128)(2,1)S(1)}, bf16[3584,3584]{1,0:T(8,128)(2,1)S(1)}, bf16[8,3584]{1,0:T(8,128)(2,1)S(1)}, bf16[8,3584]{1,0:T(8,128)(2,1)S(1)}) custom-call(s32[64]{0:T(128)} %lens_hbm.1, bf16[8,3584]{1,0:T(8,128)(2,1)} %x_hbm.1, f32[1,128]{1,0:T(1,128)} %constant.2.clone.freq_hbm, ...), custom_call_target="tpu_custom_call" | custom-call | tf_op jit(solution)/shard_map/gather_attend/pallas_call | solution.py:247
  98.9 5.0 %finish.1 = (bf16[8,3584]{1,0:T(8,128)(2,1)}, bf16[8,128,16,128]{3,2,1,0:T(8,128)(2,1)}, bf16[8,128,16,128]{3,2,1,0:T(8,128)(2,1)}) custom-call(bf16[8,128,16,128]{3,2,1,0:T(8,128)(2,1)S(1)} %get-tuple-element.11.kbuf, bf16[8,128,16,128]{3,2,1,0:T(8,128)(2,1)S(1)} %get-tuple-element.12.vbuf, bf16[3584,3584]{1,0:T(8,128)(2,1)S(1)} %get-tuple-element.13.wo_ref, ...), custom_call_target="tpu_custom_call" | custom-call | tf_op jit(solution)/shard_map/finish/pallas_call | solution.py:290

commit v5 on v3

--- a/solution.py
+++ b/solution.py
@@ -74,9 +74,6 @@
         src, c = blocks[t]
         return pltpu.make_async_copy(src.at[:, pl.ds(c * cols, cols)], wbuf.at[t % wbuf.shape[0]], wsem.at[t % wbuf.shape[0]])
 
-    for t in range(wbuf.shape[0]):
-        weight_copy(t).start()
-
     pltpu.make_async_copy(block(k_hbm, me, 0, rows), span(kbuf, me, 0, rows), k_recv.at[me]).start()
     for part in range(parts):
         pltpu.make_async_copy(block(v_hbm, me, part, part_rows), span(vbuf, me, part, part_rows), v_recv.at[me, part]).start()
@@ -87,6 +84,9 @@
     for part in range(parts):
         for t in range(1, n):
             values_copy(place(t, 1), me, part).start()
+
+    for t in range(wbuf.shape[0]):
+        weight_copy(t).start()
 
     for copy in smalls:
         copy.wait()
@@ -195,18 +195,22 @@
         copy.start()
     cols = 512
 
+    def y_copy(c):
+        span = pl.ds(pl.multiple_of(c * cols, cols), cols)
+        return pltpu.make_async_copy(y_ref.at[:, span], y_out.at[:, span], y_sem.at[c])
+
     def project(c, carry):
         span = pl.ds(pl.multiple_of(c * cols, cols), cols)
         out = jnp.dot(att_ref[...], wo_ref[:, span], preferred_element_type=jnp.float32)
         y_ref[:, span] = (x_ref[:, span].astype(jnp.float32) + out).astype(jnp.bfloat16)
+        y_copy(c).start()
         return carry
 
     lax.fori_loop(0, y_ref.shape[1] // cols, project, 0)
-    y_copy = pltpu.make_async_copy(y_ref, y_out, y_sem)
-    y_copy.start()
     for copy in copies:
         copy.wait()
-    y_copy.wait()
+    for c in range(y_ref.shape[1] // cols):
+        y_copy(c).wait()
 
 
 def solution(mesh):
@@ -282,7 +286,7 @@
             ],
             in_specs=[vmem] * 5,
             out_specs=[hbm] * 3,
-            scratch_shapes=[pltpu.VMEM(x_tok.shape, bf16), pltpu.SemaphoreType.DMA((2, rows)), pltpu.SemaphoreType.DMA],
+            scratch_shapes=[pltpu.VMEM(x_tok.shape, bf16), pltpu.SemaphoreType.DMA((2, rows)), pltpu.SemaphoreType.DMA((d_model // 512,))],
             compiler_params=pltpu.CompilerParams(vmem_limit_bytes=28 * 1024 * 1024),
             name='finish',
         )(*[pltpu.with_memory_space_constraint(a, pltpu.VMEM) for a in (kbuf, vbuf, wo, att, x_near)])

time: 103 us -> 104 us (level)
  no operation moved by 1% of the time
where the time goes in v5:
time: 104 us; the launch traced here: 103 us
  Pallas kernels  103 us (99%)
    pallas_call x1, Pallas kernels, per_device(): pl.pallas_call(functools.partial(gather_kernel, n, kv_heads), out_shape=[...  97.8 us
    pallas_call x1, Pallas kernels, per_device(): pl.pallas_call(finish_kernel, out_shape=[jax.ShapeDtypeStruct(x_tok.shape...  5.03 us

profile of v5, /device:TPU:113, one launch (start us, length us, event | category | flops | bytes accessed | tf_op | source)
XLA Modules:
  0.0 103.4 jit_solution(7231023759920419447)
XLA Ops:
  0.6 97.8 %gather_attend.1 = (bf16[8,128,16,128]{3,2,1,0:T(8,128)(2,1)S(1)}, bf16[8,128,16,128]{3,2,1,0:T(8,128)(2,1)S(1)}, bf16[3584,3584]{1,0:T(8,128)(2,1)S(1)}, bf16[8,3584]{1,0:T(8,128)(2,1)S(1)}, bf16[8,3584]{1,0:T(8,128)(2,1)S(1)}) custom-call(s32[64]{0:T(128)} %lens_hbm.1, bf16[8,3584]{1,0:T(8,128)(2,1)} %x_hbm.1, f32[1,128]{1,0:T(1,128)} %constant.2.clone.freq_hbm, ...), custom_call_target="tpu_custom_call" | custom-call | tf_op jit(solution)/shard_map/gather_attend/pallas_call | solution.py:240
  98.4 5.0 %finish.1 = (bf16[8,3584]{1,0:T(8,128)(2,1)}, bf16[8,128,16,128]{3,2,1,0:T(8,128)(2,1)}, bf16[8,128,16,128]{3,2,1,0:T(8,128)(2,1)}) custom-call(bf16[8,128,16,128]{3,2,1,0:T(8,128)(2,1)S(1)} %get-tuple-element.11.kbuf, bf16[8,128,16,128]{3,2,1,0:T(8,128)(2,1)S(1)} %get-tuple-element.12.vbuf, bf16[3584,3584]{1,0:T(8,128)(2,1)S(1)} %get-tuple-element.13.wo_ref, ...), custom_call_target="tpu_custom_call" | custom-call | tf_op jit(solution)/shard_map/finish/pallas_call | solution.py:280

commit v6 on v3

--- a/solution.py
+++ b/solution.py
@@ -11,6 +11,7 @@
 RMS_EPS = 1e-6
 ROPE_THETA = 1000000.0
 PACK = 16
+LANES = 128
 NEG = -1e30
 
 
@@ -21,7 +22,7 @@
     rows, d_model = x_ref.shape
     head = acc_ref.shape[-1]
     q_rows = acc_ref.shape[1]
-    heads = att_ref.shape[1] // head
+    heads = wq_hbm.shape[1] // head
     group = heads // kv_heads
     tiles = k_hbm.shape[1]
     block_rows = tiles * PACK
@@ -124,8 +125,10 @@
                     vnew_ref[:, r * kv_heads + i, :] = part
             else:
                 qf_ref[:, c * (cols // head) + i, :] = rotate(part)
-    wo_copy = pltpu.make_async_copy(wo_hbm, wo_ref, wo_sem)
-    wo_copy.start()
+    lane_width = wo_ref.shape[2]
+    wo_copies = [pltpu.make_async_copy(wo_hbm.at[:, pl.ds(c * lane_width, lane_width)], wo_ref.at[c], wo_sem.at[c]) for c in range(wo_ref.shape[0])]
+    for copy in wo_copies:
+        copy.start()
 
     def merged(s, sender, buf, new_ref):
         pos = lens[me * rows + s]
@@ -161,6 +164,10 @@
         acc_ref[s] += jnp.dot(p_ref[s, sender], values, preferred_element_type=jnp.float32)
         return 0
 
+    def attended_row(s):
+        att_ref[s] = acc_ref[s] / sum_ref[s]
+        return 0
+
     def keys_arrival(t, carry):
         sender = place(t, -1)
         keys_copy(sender, sender).wait_recv()
@@ -169,16 +176,21 @@
     def values_arrival(u, carry):
         part, sender = u // n, place(lax.rem(u, n), -1)
         values_copy(sender, sender, part).wait_recv()
-        return lax.fori_loop(part * part_rows, (part + 1) * part_rows, lambda s, c: values_step(s, sender), carry)
+        lax.fori_loop(part * part_rows, (part + 1) * part_rows, lambda s, c: values_step(s, sender), carry)
+
+        @pl.when(lax.rem(u, n) == n - 1)
+        def _():
+            lax.fori_loop(part * part_rows, (part + 1) * part_rows, lambda s, c: attended_row(s), carry)
+
+        return carry
 
     lax.fori_loop(0, n, keys_arrival, 0)
     lax.fori_loop(0, rows, lambda s, c: soften(s), 0)
     acc_ref[...] = jnp.zeros_like(acc_ref)
-    wo_copy.wait()
+    for copy in wo_copies:
+        copy.wait()
     lax.fori_loop(0, n * parts, values_arrival, 0)
 
-    for j in range(heads):
-        att_ref[:, j * head:(j + 1) * head] = (acc_ref[:, j, :] / sum_ref[:, j, :]).astype(jnp.bfloat16)
     for t in range(1, n):
         keys_copy(place(t, 1), me).wait_send()
         for part in range(parts):
@@ -193,11 +205,15 @@
     ]
     for copy in copies:
         copy.start()
-    cols = 512
+    strips = 4
+    cols = strips * LANES
+    heads = wo_ref.shape[1] // att_ref.shape[2]
+    attended = jnp.concatenate([att_ref[:, j, :] for j in range(heads)], axis=1).astype(jnp.bfloat16)
 
     def project(c, carry):
         span = pl.ds(pl.multiple_of(c * cols, cols), cols)
-        out = jnp.dot(att_ref[...], wo_ref[:, span], preferred_element_type=jnp.float32)
+        weights = jnp.concatenate([wo_ref[c * strips + i] for i in range(strips)], axis=1)
+        out = jnp.dot(attended, weights, preferred_element_type=jnp.float32)
         y_ref[:, span] = (x_ref[:, span].astype(jnp.float32) + out).astype(jnp.bfloat16)
         return carry
 
@@ -238,8 +254,8 @@
             out_shape=[
                 pltpu.VMEM((rows, all_tiles, PACK, head), bf16),
                 pltpu.VMEM((rows, all_tiles, PACK, head), bf16),
-                pltpu.VMEM(w_o.shape, bf16),
-                pltpu.VMEM((rows, q_cols), bf16),
+                pltpu.VMEM((w_o.shape[1] // LANES, w_o.shape[0], LANES), bf16),
+                pltpu.VMEM((rows, q_rows, head), f32),
                 pltpu.VMEM((rows, d_model), bf16),
             ],
             in_specs=[hbm] * 13,
@@ -262,7 +278,7 @@
                 pltpu.VMEM((rows, q_rows, head), f32),
                 pltpu.SemaphoreType.DMA((7,)),
                 pltpu.SemaphoreType.DMA((3,)),
-                pltpu.SemaphoreType.DMA,
+                pltpu.SemaphoreType.DMA((w_o.shape[1] // LANES,)),
                 pltpu.SemaphoreType.DMA((n,)),
                 pltpu.SemaphoreType.DMA((n,)),
                 pltpu.SemaphoreType.DMA((n, parts)),

time: 103 us -> 104 us (level)
  no operation moved by 1% of the time
where the time goes in v6:
time: 104 us; the launch traced here: 103 us
  Pallas kernels  103 us (99%)
    pallas_call x1, Pallas kernels, per_device(): pl.pallas_call(functools.partial(gather_kernel, n, kv_heads), out_shape=[...  97.8 us
    pallas_call x1, Pallas kernels, per_device(): pl.pallas_call(finish_kernel, out_shape=[jax.ShapeDtypeStruct(x_tok.shape...  5.02 us

profile of v6, /device:TPU:113, one launch (start us, length us, event | category | flops | bytes accessed | tf_op | source)
XLA Modules:
  0.0 103.5 jit_solution(12545073762588829660)
XLA Ops:
  0.6 97.8 %gather_attend.1 = (bf16[8,128,16,128]{3,2,1,0:T(8,128)(2,1)S(1)}, bf16[8,128,16,128]{3,2,1,0:T(8,128)(2,1)S(1)}, bf16[28,3584,128]{2,1,0:T(8,128)(2,1)S(1)}, f3...) custom-call(s32[64]{0:T(128)} %lens_hbm.1, bf16[8,3584]{1,0:T(8,128)(2,1)} %x_hbm.1, f32[1,128]{1,0:T(1,128)} %constant.2.clone.freq_hbm, ...), custom_call_target="tpu_custom_call" | custom-call | tf_op jit(solution)/shard_map/gather_attend/pallas_call | solution.py:252
  98.4 5.0 %finish.1 = (bf16[8,3584]{1,0:T(8,128)(2,1)}, bf16[8,128,16,128]{3,2,1,0:T(8,128)(2,1)}, bf16[8,128,16,128]{3,2,1,0:T(8,128)(2,1)}) custom-call(bf16[8,128,16,128]{3,2,1,0:T(8,128)(2,1)S(1)} %get-tuple-element.11.kbuf, bf16[8,128,16,128]{3,2,1,0:T(8,128)(2,1)S(1)} %get-tuple-element.12.vbuf, bf16[28,3584,128]{2,1,0:T(8,128)(2,1)S(1)} %get-tuple-element.13.wo_ref, ...), custom_call_target="tpu_custom_call" | custom-call | tf_op jit(solution)/shard_map/finish/pallas_call | solution.py:292

commit v7 on v6

--- a/solution.py
+++ b/solution.py
@@ -18,7 +18,7 @@
 def gather_kernel(n, kv_heads, lens_hbm, x_hbm, freq_hbm, gain_hbm, wq_hbm, bq_hbm, wk_hbm, bk_hbm, wv_hbm, bv_hbm, wo_hbm, k_hbm, v_hbm,
                   kbuf, vbuf, wo_ref, att_ref, x_ref,
                   lens, freq_ref, gain_ref, bq_ref, bk_ref, bv_ref, wbuf, h_ref, qf_ref, knew_ref, vnew_ref, s_ref, p_ref, acc_ref, sum_ref,
-                  small_sem, wsem, wo_sem, k_send, k_recv, v_send, v_recv):
+                  small_sem, wsem, wo_sem, k_send, k_recv, v_send, v_recv, far_sem):
     rows, d_model = x_ref.shape
     head = acc_ref.shape[-1]
     q_rows = acc_ref.shape[1]
@@ -35,7 +35,9 @@
     parts = v_recv.shape[1]
     part_rows = rows // parts
 
-    fars = sorted(range(1, chips), key=lambda f: -min(f, chips - f))
+    fars = sorted(range(1, chips), key=lambda f: min(f, chips - f))
+    near = 2 * sum(min(f, chips - f) == 1 for f in fars) + 2
+    assert chips == 4 and near == 6
 
     def place(t, way):
         far = sum(jnp.where(t // 2 == k + 1, f, 0) for k, f in enumerate(fars))
@@ -58,7 +60,7 @@
             recv_sem=v_recv.at[sender, part], device_id={'cp': to}, device_id_type=pl.DeviceIdType.MESH)
 
     barrier = pltpu.get_barrier_semaphore()
-    for t in range(1, n):
+    for t in range(1, near):
         pl.semaphore_signal(barrier, inc=1, device_id={'cp': place(t, 1)}, device_id_type=pl.DeviceIdType.MESH)
 
     smalls = [
@@ -82,8 +84,13 @@
     for part in range(parts):
         pltpu.make_async_copy(block(v_hbm, me, part, part_rows), span(vbuf, me, part, part_rows), v_recv.at[me, part]).start()
 
-    pl.semaphore_wait(barrier, n - 1)
-    for t in range(1, n):
+    pl.semaphore_wait(barrier, near - 1)
+    for t in range(1, near):
+        keys_copy(place(t, 1), me).start()
+    for t in range(2, near, 2):
+        pl.semaphore_signal(far_sem, inc=1, device_id={'cp': place(t, 1)}, device_id_type=pl.DeviceIdType.MESH)
+    pl.semaphore_wait(far_sem, near // 2 - 1)
+    for t in range(near, n):
         keys_copy(place(t, 1), me).start()
     for part in range(parts):
         for t in range(1, n):
@@ -283,6 +290,7 @@
                 pltpu.SemaphoreType.DMA((n,)),
                 pltpu.SemaphoreType.DMA((n, parts)),
                 pltpu.SemaphoreType.DMA((n, parts)),
+                pltpu.SemaphoreType.REGULAR,
             ],
             compiler_params=pltpu.CompilerParams(collective_id=0, has_side_effects=True, vmem_limit_bytes=28 * 1024 * 1024),
             name='gather_attend',

time: 104 us -> 104 us (level)
  no operation moved by 1% of the time
where the time goes in v7:
time: 104 us
  Pallas kernels  103 us (99%)
    pallas_call x1, Pallas kernels, per_device(): pl.pallas_call(functools.partial(gather_kernel, n, kv_heads), out_shape=[...  98.2 us
    pallas_call x1, Pallas kernels, per_device(): pl.pallas_call(finish_kernel, out_shape=[jax.ShapeDtypeStruct(x_tok.shape...  5.02 us

profile of v7, /device:TPU:113, one launch (start us, length us, event | category | flops | bytes accessed | tf_op | source)
XLA Modules:
  0.0 103.8 jit_solution(1879164474905310926)
XLA Ops:
  0.6 98.2 %gather_attend.1 = (bf16[8,128,16,128]{3,2,1,0:T(8,128)(2,1)S(1)}, bf16[8,128,16,128]{3,2,1,0:T(8,128)(2,1)S(1)}, bf16[28,3584,128]{2,1,0:T(8,128)(2,1)S(1)}, f3...) custom-call(s32[64]{0:T(128)} %lens_hbm.1, bf16[8,3584]{1,0:T(8,128)(2,1)} %x_hbm.1, f32[1,128]{1,0:T(1,128)} %constant.2.clone.freq_hbm, ...), custom_call_target="tpu_custom_call" | custom-call | tf_op jit(solution)/shard_map/gather_attend/pallas_call | solution.py:259
  98.8 5.0 %finish.1 = (bf16[8,3584]{1,0:T(8,128)(2,1)}, bf16[8,128,16,128]{3,2,1,0:T(8,128)(2,1)}, bf16[8,128,16,128]{3,2,1,0:T(8,128)(2,1)}) custom-call(bf16[8,128,16,128]{3,2,1,0:T(8,128)(2,1)S(1)} %get-tuple-element.11.kbuf, bf16[8,128,16,128]{3,2,1,0:T(8,128)(2,1)S(1)} %get-tuple-element.12.vbuf, bf16[28,3584,128]{2,1,0:T(8,128)(2,1)S(1)} %get-tuple-element.13.wo_ref, ...), custom_call_target="tpu_custom_call" | custom-call | tf_op jit(solution)/shard_map/finish/pallas_call | solution.py:300

commit v8 on v7

--- a/solution.py
+++ b/solution.py
@@ -43,6 +43,8 @@
         far = sum(jnp.where(t // 2 == k + 1, f, 0) for k, f in enumerate(fars))
         return lax.rem(chip + way * far + chips, chips) * 2 + lax.rem(core + t, 2)
 
+    values_order = [*range(near, n), *range(1, near)]
+
     def block(ref, owner, part, count):
         return ref.at[pl.ds(owner * rows + part * count, count)]
 
@@ -93,7 +95,7 @@
     for t in range(near, n):
         keys_copy(place(t, 1), me).start()
     for part in range(parts):
-        for t in range(1, n):
+        for t in values_order:
             values_copy(place(t, 1), me, part).start()
 
     for copy in smalls:
@@ -181,7 +183,7 @@
         return lax.fori_loop(0, rows, lambda s, c: keys_step(s, sender), carry)
 
     def values_arrival(u, carry):
-        part, sender = u // n, place(lax.rem(u, n), -1)
+        part, sender = u // n, place(lax.rem(lax.rem(u, n) + near, n), -1)
         values_copy(sender, sender, part).wait_recv()
         lax.fori_loop(part * part_rows, (part + 1) * part_rows, lambda s, c: values_step(s, sender), carry)
 

time: 104 us -> 103 us (level)
  no operation moved by 1% of the time
where the time goes in v8:
time: 103 us
  Pallas kernels  103 us (100%)
    pallas_call x1, Pallas kernels, per_device(): pl.pallas_call(functools.partial(gather_kernel, n, kv_heads), out_shape=[...  97.6 us
    pallas_call x1, Pallas kernels, per_device(): pl.pallas_call(finish_kernel, out_shape=[jax.ShapeDtypeStruct(x_tok.shape...  5.02 us

profile of v8, /device:TPU:113, one launch (start us, length us, event | category | flops | bytes accessed | tf_op | source)
XLA Modules:
  0.0 103.3 jit_solution(1080937815181472524)
XLA Ops:
  0.6 97.6 %gather_attend.1 = (bf16[8,128,16,128]{3,2,1,0:T(8,128)(2,1)S(1)}, bf16[8,128,16,128]{3,2,1,0:T(8,128)(2,1)S(1)}, bf16[28,3584,128]{2,1,0:T(8,128)(2,1)S(1)}, f3...) custom-call(s32[64]{0:T(128)} %lens_hbm.1, bf16[8,3584]{1,0:T(8,128)(2,1)} %x_hbm.1, f32[1,128]{1,0:T(1,128)} %constant.2.clone.freq_hbm, ...), custom_call_target="tpu_custom_call" | custom-call | tf_op jit(solution)/shard_map/gather_attend/pallas_call | solution.py:261
  98.2 5.0 %finish.1 = (bf16[8,3584]{1,0:T(8,128)(2,1)}, bf16[8,128,16,128]{3,2,1,0:T(8,128)(2,1)}, bf16[8,128,16,128]{3,2,1,0:T(8,128)(2,1)}) custom-call(bf16[8,128,16,128]{3,2,1,0:T(8,128)(2,1)S(1)} %get-tuple-element.11.kbuf, bf16[8,128,16,128]{3,2,1,0:T(8,128)(2,1)S(1)} %get-tuple-element.12.vbuf, bf16[28,3584,128]{2,1,0:T(8,128)(2,1)S(1)} %get-tuple-element.13.wo_ref, ...), custom_call_target="tpu_custom_call" | custom-call | tf_op jit(solution)/shard_map/finish/pallas_call | solution.py:302
